TPU v7x, 256 devices: a whole 4x4x8 slice. The times are simulated.
256 devices in a mesh: dp: 32 (over y, x, core), seq: 8 (over z).
Axes of the slice: x: 4, y: 4, z: 8, core: 2. Of those that a mesh axis runs over, the one named last changes fastest.
Arguments:
- query_rows: bfloat16 [32, 1024, 3072], P('dp', 'seq'), may hold values from -6 to 6
- key_rows: bfloat16 [32, 1024, 3072], P('dp', 'seq'), may hold values from -6 to 6
- value_rows: bfloat16 [32, 1024, 3072], P('dp', 'seq'), may hold values from -6 to 6
- out_grad: bfloat16 [32, 1024, 6144], P('dp', 'seq'), may hold values from -54 to 54
- clip_lengths: int32 [32, 4], P('dp'), may hold values from 1 to 512, 1024 in all within a row
- out_weight: bfloat16 [3072, 6144], P('seq'), may hold values from -0.109375 to 0.109375
- query_gain: float32 [128], replicated, may hold values from 0.1 to 1.9
- key_gain: float32 [128], replicated, may hold values from 0.1 to 1.9
Outputs:
- query_grad: bfloat16 [32, 1024, 3072], P('dp', 'seq')
- key_grad: bfloat16 [32, 1024, 3072], P('dp', 'seq')
- value_grad: bfloat16 [32, 1024, 3072], P('dp', 'seq')
- weight_grad: float32 [3072, 6144], P('seq', 'dp')
- querygain_grad: float32 [128], replicated
- keygain_grad: float32 [128], replicated
- grad_norm: float32 [], replicated
Inputs may be any that keep to these rules, and one draw needn't show every extreme that they name: `clip_lengths`: the token counts of each group's clips sum to 1024.
All inputs are finite; a program needn't handle non-finite values.
Results may differ from a plain program's by a relative error of at most 0.015.
Values may be sent and summed in bfloat16 or wider, within the bound.
A program may use at most 128 MiB of HBM per device.

v0:
```python
import jax
import jax.numpy as jnp
from jax import lax
from jax.sharding import Mesh
from jax.sharding import PartitionSpec as P

HEAD_DIM = 128
MAX_NORM = 768
DP = ("dp_0", "dp_1", "dp_2")
DP_SEQ = ("dp_0", "dp_1", "dp_2", "seq")
EPS = 1e-06


def one_axis_at_a_time(array, axes):
    for axis in axes:
        array = lax.psum(array, axis)
    return array


def segment_ids(lengths, total):
    ends = jnp.cumsum(lengths)
    places = jnp.arange(total, dtype=jnp.int32)
    return jnp.sum((places[:, None] >= ends[None, :]).astype(jnp.int32), axis=1)


def norm_rows(rows, gain):
    wide = rows.astype(jnp.float32)
    inverse = lax.rsqrt(jnp.mean(wide * wide, axis=-1, keepdims=True) + EPS)
    unit = wide * inverse
    return (unit, inverse, (unit * gain).astype(jnp.bfloat16))


def norm_back(unit, inverse, gain, d_norm):
    gain_part = jnp.sum(unit * d_norm, axis=(0, 1))
    d_unit = d_norm * gain
    d_rows = inverse * (d_unit - unit * jnp.mean(unit * d_unit, axis=-1, keepdims=True))
    return (d_rows.astype(jnp.bfloat16), gain_part)


def local(
    query_rows, key_rows, value_rows, out_grad, clip_lengths, out_weight, query_gain, key_gain
):
    query, keys, values = (
        lax.all_to_all(query_rows[0], "seq", split_axis=1, concat_axis=0, tiled=True),
        lax.all_to_all(key_rows[0], "seq", split_axis=1, concat_axis=0, tiled=True),
        lax.all_to_all(value_rows[0], "seq", split_axis=1, concat_axis=0, tiled=True),
    )
    total = query.shape[0]
    heads = query.shape[1] // HEAD_DIM
    width = heads * HEAD_DIM
    scale = HEAD_DIM ** (-0.5)
    block = min(512, total)
    blocks = total // block
    seg = segment_ids(clip_lengths[0], total)
    q_unit, q_inv, q_norm = norm_rows(query.reshape(total, heads, HEAD_DIM), query_gain)
    k_unit, k_inv, k_norm = norm_rows(keys.reshape(total, heads, HEAD_DIM), key_gain)
    values3 = values.reshape(total, heads, HEAD_DIM)

    def forward_block(index):
        start = index * block
        query_block = lax.dynamic_slice_in_dim(q_norm, start, block, 0)
        seg_block = lax.dynamic_slice_in_dim(seg, start, block, 0)
        scores = (
            jnp.einsum("qhd,khd->hqk", query_block, k_norm, preferred_element_type=jnp.float32)
            * scale
        )
        same = seg_block[:, None] == seg[None, :]
        expo = jnp.where(same[None], jnp.exp(scores), 0.0)
        probs = (expo / jnp.sum(expo, axis=-1, keepdims=True)).astype(jnp.bfloat16)
        attn_out = jnp.einsum("hqk,khd->qhd", probs, values3, preferred_element_type=jnp.float32)
        return (probs, attn_out.astype(jnp.bfloat16))

    probs_all, attn_blocks = lax.map(forward_block, jnp.arange(blocks, dtype=jnp.int32))
    attn_flat = attn_blocks.reshape(total, width)
    out_full = lax.all_gather(out_grad[0], "seq", axis=0, tiled=True)
    weight_part = jnp.dot(attn_flat.T, out_full, preferred_element_type=jnp.float32)
    d_attn = jnp.dot(out_full, out_weight.T, preferred_element_type=jnp.float32).astype(
        jnp.bfloat16
    )
    d_attn3 = d_attn.reshape(total, heads, HEAD_DIM)

    def backward_block(carry, items):
        d_key, d_value = carry
        probs, index = items
        start = index * block
        attn_grad = lax.dynamic_slice_in_dim(d_attn3, start, block, 0)
        query_block = lax.dynamic_slice_in_dim(q_norm, start, block, 0)
        d_probs = jnp.einsum("qhd,khd->hqk", attn_grad, values3, preferred_element_type=jnp.float32)
        probs32 = probs.astype(jnp.float32)
        row_sum = jnp.sum(probs32 * d_probs, axis=-1, keepdims=True)
        d_scores = (probs32 * (d_probs - row_sum) * scale).astype(jnp.bfloat16)
        d_value = d_value + jnp.einsum(
            "hqk,qhd->khd", probs, attn_grad, preferred_element_type=jnp.float32
        )
        d_key = d_key + jnp.einsum(
            "hqk,qhd->khd", d_scores, query_block, preferred_element_type=jnp.float32
        )
        d_query = jnp.einsum("hqk,khd->qhd", d_scores, k_norm, preferred_element_type=jnp.float32)
        return ((d_key, d_value), d_query)

    empty = jnp.zeros((total, heads, HEAD_DIM), jnp.float32)
    (d_knorm, d_value32), d_query_blocks = lax.scan(
        backward_block, (empty, empty), (probs_all, jnp.arange(blocks, dtype=jnp.int32))
    )
    d_qnorm = d_query_blocks.reshape(total, heads, HEAD_DIM)
    query_grad, q_gain_part = norm_back(q_unit, q_inv, query_gain, d_qnorm)
    key_grad, k_gain_part = norm_back(k_unit, k_inv, key_gain, d_knorm)
    value_grad = d_value32.astype(jnp.bfloat16)
    query_back, key_back, value_back = (
        lax.all_to_all(
            query_grad.reshape(total, width), "seq", split_axis=0, concat_axis=1, tiled=True
        ),
        lax.all_to_all(
            key_grad.reshape(total, width), "seq", split_axis=0, concat_axis=1, tiled=True
        ),
        lax.all_to_all(
            value_grad.reshape(total, width), "seq", split_axis=0, concat_axis=1, tiled=True
        ),
    )
    weight_shard = lax.psum_scatter(
        weight_part.astype(jnp.bfloat16), DP, scatter_dimension=1, tiled=True
    ).astype(jnp.float32)
    local_squares = jnp.sum(weight_shard * weight_shard)
    qgain_raw, kgain_raw = (
        one_axis_at_a_time(q_gain_part, DP_SEQ),
        one_axis_at_a_time(k_gain_part, DP_SEQ),
    )
    weight_squares = one_axis_at_a_time(local_squares, DP_SEQ)
    squares = weight_squares + jnp.sum(qgain_raw * qgain_raw) + jnp.sum(kgain_raw * kgain_raw)
    grad_norm = jnp.sqrt(squares)
    factor = jnp.minimum(jnp.float32(1.0), MAX_NORM / (grad_norm + EPS))
    return (
        query_back[None],
        key_back[None],
        value_back[None],
        weight_shard * factor,
        qgain_raw * factor,
        kgain_raw * factor,
        grad_norm,
    )


def solution(mesh):
    torus = Mesh(mesh.devices.reshape(4, 4, 2, mesh.shape["seq"]), ("dp_0", "dp_1", "dp_2", "seq"))
    return jax.shard_map(
        local,
        mesh=torus,
        in_specs=(
            P(DP, "seq", None),
            P(DP, "seq", None),
            P(DP, "seq", None),
            P(DP, "seq", None),
            P(DP, None),
            P("seq", None),
            P(),
            P(),
        ),
        out_specs=(
            P(DP, "seq", None),
            P(DP, "seq", None),
            P(DP, "seq", None),
            P("seq", DP),
            P(),
            P(),
            P(),
        ),
        check_vma=False,
    )
```

profile of v0, /device:TPU:32, one launch (start us, length us, event | category | flops | bytes accessed | tf_op | source)
XLA Modules:
  0.0 430.5 jit_solution(6281215837916845542)
XLA Ops:
  9.5 8.6 %all-to-all-start = ((bf16[128,8,384]{0,2,1:T(8,128)(2,1)}), bf16[128,8,384]{0,2,1:T(8,128)(2,1)S(1)}, u32[]{:S(2)}, u32[]{:S(2)}) async-start(bf16[128,8,384]{0,2,1:T(8,128)(2,1)} %bitcast.4), calls=%async_computation | async-start | bytes 1572864 | tf_op jit(solution)/shard_map/all_to_all | solution.py:44
  19.2 26.2 %all-to-all-done = bf16[128,8,384]{0,2,1:T(8,128)(2,1)S(1)} async-done(((bf16[128,8,384]{0,2,1:T(8,128)(2,1)}), bf16[128,8,384]{0,2,1:T(8,128)(2,1)S(1)}, u32[]{:S(2)}, u32[]{:S(2)}) %all-to-all-start) | async-done | bytes 786464 | tf_op jit(solution)/shard_map/all_to_all | solution.py:44
  45.4 5.8 %all-to-all-start.1 = ((bf16[128,8,384]{0,2,1:T(8,128)(2,1)}), bf16[128,8,384]{0,2,1:T(8,128)(2,1)S(1)}, u32[]{:S(2)}, u32[]{:S(2)}) async-start(bf16[128,8,384]{0,2,1:T(8,128)(2,1)} %bitcast.8), calls=%async_computation.1 | async-start | bytes 1572864 | tf_op jit(solution)/shard_map/all_to_all | solution.py:45
  52.3 30.0 %all-to-all-done.1 = bf16[128,8,384]{0,2,1:T(8,128)(2,1)S(1)} async-done(((bf16[128,8,384]{0,2,1:T(8,128)(2,1)}), bf16[128,8,384]{0,2,1:T(8,128)(2,1)S(1)}, u32[]{:S(2)}, u32[]{:S(2)}) %all-to-all-start.1) | async-done | bytes 786464 | tf_op jit(solution)/shard_map/all_to_all | solution.py:45
  82.4 5.3 %all-to-all-start.2 = ((bf16[128,8,384]{0,2,1:T(8,128)(2,1)}), bf16[128,8,384]{0,2,1:T(8,128)(2,1)}, u32[]{:S(2)}, u32[]{:S(2)}) async-start(bf16[128,8,384]{0,2,1:T(8,128)(2,1)} %bitcast.10), calls=%async_computation.2 | async-start | bytes 1572864 | tf_op jit(solution)/shard_map/all_to_all | solution.py:46
  99.7 19.1 %all-to-all-done.2 = bf16[128,8,384]{0,2,1:T(8,128)(2,1)} async-done(((bf16[128,8,384]{0,2,1:T(8,128)(2,1)}), bf16[128,8,384]{0,2,1:T(8,128)(2,1)}, u32[]{:S(2)}, u32[]{:S(2)}) %all-to-all-start.2) | async-done | bytes 786464 | tf_op jit(solution)/shard_map/all_to_all | solution.py:46
  128.8 21.1 %while.27 = (s32[]{:T(128)}, bf16[2,3,512,1024]{3,2,1,0:T(8,128)(2,1)}, bf16[2,512,3,128]{3,1,2,0:T(8,128)(2,1)}, s32[2]{0:T(128)S(1)}, s32[1024]{0:T(1024)S(1)}...) while((s32[]{:T(128)}, ...), condition=%wide.region_6.7_spmd, body=%wide.region_4.6_spmd.sunk | while | flops 817035776 | bytes 85746000 | solution.py:73
  156.8 32.1 %all-gather.3.cloned.1.call-done = bf16[1,1024,6144]{2,1,0:T(8,128)(2,1)} async-done(((bf16[1,128,6144]{2,1,0:T(8,128)(2,1)}), bf16[1,1024,6144]{2,1,0:T(8,128)(2,1)}) %all-gather.3.cloned.1.call-update) | async-done | bytes 12582928 | tf_op jit(solution)/shard_map/all_gather | solution.py:75
  188.9 11.4 %fusion.42 = bf16[384,6144]{0,1:T(8,128)(2,1)} fusion(bf16[1024,384]{0,1:T(8,128)(2,1)} %bitcast.161, bf16[1,1024,6144]{2,1,0:T(8,128)(2,1)} %all-gather.3.cloned.1.call-done), kind=kOutput, calls=%fused_computation.45 | convolution fusion | flops 4834197504 | bytes 18087936 | tf_op jit(solution)/shard_map/dot_general | solution.py:76
  200.3 10.4 %fusion.48 = bf16[1024,384]{0,1:T(8,128)(2,1)} fusion(bf16[384,6144]{1,0:T(8,128)(2,1)} %param.17, bf16[1,1024,6144]{2,1,0:T(8,128)(2,1)} %all-gather.3.cloned.1.call-done), kind=kOutput, calls=%fused_computation.62 | convolution fusion | flops 4832231424 | bytes 18087936 | tf_op jit(solution)/shard_map/dot_general | solution.py:77
  210.8 57.7 %while.28 = (s32[]{:T(128)}, f32[1024,3,128]{0,2,1:T(8,128)}, f32[1024,3,128]{0,2,1:T(8,128)S(1)}, f32[2,512,3,128]{3,1,2,0:T(8,128)}, s32[2]{0:T(128)S(1)}, /*i...) while((s32[]{:T(128)}, f32[1024,3,128]{0,2,1:T(8,128)}, ...), condition=%wide.region_9.10_spmd.clone, body=%wide.region_7.9_spmd.clone.sunk | while | flops 1634210816 | bytes 57019604 | solution.py:102
  212.0 5.0 %fusion.83 = f32[3,512,1024]{2,1,0:T(8,128)} fusion(bf16[1024,3,128]{2,0,1:T(8,128)(2,1)} %get-tuple-element.549, bf16[1024,3,128]{0,2,1:T(8,128)(2,1)} %get-tuple-element.548, s32[]{:T(128)S(6)} %select_n.24), kind=kOutput, calls=%fused_computation.30.clone.1 | convolution fusion | flops 402653184 | bytes 7471108 | tf_op jit(solution)/shard_map/while/body/eval_jaxpr/qhd,khd->hqk/dot_general | solution.py:88
  217.0 10.2 %bitcast_add_fusion.4 = f32[1024,3,128]{0,2,1:T(8,128)} fusion(f32[1024,3,128]{0,2,1:T(8,128)} %get-tuple-element.528, f32[3,512,1024]{2,1,0:T(8,128)} %fusion.83, bf16[2,3,512,1024]{3,2,1,0:T(8,128)(2,1)} %get-tuple-element.547, s32[]{:T(128)} %get-tuple-element.527, pred[]{:T(512)S(6)} %compare.3, bf16[1024,3,128]{0,2,1:T(8,128)(2,1)} %get-tuple-element.546, ...), kind=kOutput, calls=%fused_computation.26.clone.1 | convolution fusion | flops 414452224 | bytes 22414340 | tf_op jit(solution)/shard_map/while/body/eval_jaxpr/hqk,qhd->khd/dot_general | solution.py:95
  227.2 9.7 %fusion.84 = f32[2,512,3,128]{3,1,2,0:T(8,128)} fusion(f32[2,512,3,128]{3,1,2,0:T(8,128)} %get-tuple-element.530, s32[]{:T(128)} %get-tuple-element.527, bf16[1024,3,128]{2,0,1:T(8,128)(2,1)} %get-tuple-element.550, f32[3,512,1024]{2,1,0:T(8,128)} %fusion.83, bf16[2,3,512,1024]{3,2,1,0:T(8,128)(2,1)} %get-tuple-element.547), kind=kOutput, calls=%fused_computation.28.clone.1 | convolution fusion | flops 413665792 | bytes 20448768 | tf_op jit(solution)/shard_map/while/body/eval_jaxpr/hqk,khd->qhd/dot_general | solution.py:98
  246.1 10.1 %bitcast_add_fusion.4 = f32[1024,3,128]{0,2,1:T(8,128)} fusion(f32[1024,3,128]{0,2,1:T(8,128)} %get-tuple-element.528, f32[3,512,1024]{2,1,0:T(8,128)} %fusion.83, bf16[2,3,512,1024]{3,2,1,0:T(8,128)(2,1)} %get-tuple-element.547, s32[]{:T(128)} %get-tuple-element.527, pred[]{:T(512)S(6)} %compare.3, bf16[1024,3,128]{0,2,1:T(8,128)(2,1)} %get-tuple-element.546, ...), kind=kOutput, calls=%fused_computation.26.clone.1 | convolution fusion | flops 414452224 | bytes 22414340 | tf_op jit(solution)/shard_map/while/body/eval_jaxpr/hqk,qhd->khd/dot_general | solution.py:95
  256.2 9.3 %fusion.84 = f32[2,512,3,128]{3,1,2,0:T(8,128)} fusion(f32[2,512,3,128]{3,1,2,0:T(8,128)} %get-tuple-element.530, s32[]{:T(128)} %get-tuple-element.527, bf16[1024,3,128]{2,0,1:T(8,128)(2,1)} %get-tuple-element.550, f32[3,512,1024]{2,1,0:T(8,128)} %fusion.83, bf16[2,3,512,1024]{3,2,1,0:T(8,128)(2,1)} %get-tuple-element.547), kind=kOutput, calls=%fused_computation.28.clone.1 | convolution fusion | flops 413665792 | bytes 20448768 | tf_op jit(solution)/shard_map/while/body/eval_jaxpr/hqk,khd->qhd/dot_general | solution.py:98
  289.5 6.7 %all-to-all-start.3 = ((bf16[8,128,384]{1,2,0:T(8,128)(2,1)}), bf16[8,128,384]{1,2,0:T(8,128)(2,1)}, u32[]{:S(2)}, u32[]{:S(2)}) async-start(bf16[8,128,384]{1,2,0:T(8,128)(2,1)} %fusion.47), calls=%async_computation.3 | async-start | bytes 1572864 | tf_op jit(solution)/shard_map/all_to_all | solution.py:110
  300.3 17.9 %all-to-all-done.3 = bf16[8,128,384]{1,2,0:T(8,128)(2,1)} async-done(((bf16[8,128,384]{1,2,0:T(8,128)(2,1)}), bf16[8,128,384]{1,2,0:T(8,128)(2,1)}, u32[]{:S(2)}, u32[]{:S(2)}) %all-to-all-start.3) | async-done | bytes 786464 | tf_op jit(solution)/shard_map/all_to_all | solution.py:110
  324.8 18.6 %all-to-all-done.4 = bf16[8,128,384]{2,1,0:T(8,128)(2,1)S(1)} async-done(((bf16[8,128,384]{2,1,0:T(8,128)(2,1)}), bf16[8,128,384]{2,1,0:T(8,128)(2,1)S(1)}, u32[]{:S(2)}, u32[]{:S(2)}) %all-to-all-start.4) | async-done | bytes 786464 | tf_op jit(solution)/shard_map/all_to_all | solution.py:113
  343.4 5.5 %all-to-all-start.5 = ((bf16[8,128,384]{2,1,0:T(8,128)(2,1)}), bf16[8,128,384]{2,1,0:T(8,128)(2,1)}, u32[]{:S(2)}, u32[]{:S(2)}) async-start(bf16[8,128,384]{2,1,0:T(8,128)(2,1)} %copy.165), calls=%async_computation.5 | async-start | bytes 1572864 | tf_op jit(solution)/shard_map/all_to_all | solution.py:116
  357.5 11.9 %all-to-all-done.5 = bf16[8,128,384]{2,1,0:T(8,128)(2,1)} async-done(((bf16[8,128,384]{2,1,0:T(8,128)(2,1)}), bf16[8,128,384]{2,1,0:T(8,128)(2,1)}, u32[]{:S(2)}, u32[]{:S(2)}) %all-to-all-start.5) | async-done | bytes 786464 | tf_op jit(solution)/shard_map/all_to_all | solution.py:116
  373.6 13.2 %all-reduce.2 = (f32[]{:T(128)}, f32[128]{0:T(128)S(1)}, f32[128]{0:T(128)S(1)}) all-reduce(f32[]{:T(128)} %fusion.51, f32[128]{0:T(128)S(1)} %multiply_reduce_fusion.1, f32[128]{0:T(128)S(1)} %get-tuple-element.303), channel_id=1, replica_groups=mesh['dp_0'=4,'dp_1'=4,'dp_2'=2,'seq'=8] {'dp_0'}, use_global_device_ids=true, to_apply=%region_14.15 | all-reduce | flops 257 | bytes 2056 | tf_op jit(solution)/shard_map/psum | solution.py:16
  386.9 11.0 %all-reduce.1 = (f32[]{:T(128)}, f32[128]{0:T(128)S(1)}, f32[128]{0:T(128)S(1)}) all-reduce(f32[]{:T(128)} %get-tuple-element.347, f32[128]{0:T(128)S(1)} %get-tuple-element.348, f32[128]{0:T(128)S(1)} %get-tuple-element.349), channel_id=1, replica_groups=mesh['dp_0'=4,'dp_1'=4,'dp_2'=2,'seq'=8] {'dp_1'}, use_global_device_ids=true, to_apply=%region_15.16 | all-reduce | flops 257 | bytes 2056 | tf_op jit(solution)/shard_map/psum | solution.py:16
  401.0 16.2 %all-reduce = (f32[]{:T(128)}, f32[128]{0:T(128)S(1)}, f32[128]{0:T(128)S(1)}) all-reduce(f32[]{:T(128)} %get-tuple-element.350, f32[128]{0:T(128)S(1)} %get-tuple-element.351, f32[128]{0:T(128)S(1)} %get-tuple-element.352), channel_id=1, replica_groups=mesh['dp_0'=4,'dp_1'=4,'dp_2'=2,'seq'=8] {'seq'}, use_global_device_ids=true, to_apply=%region_17.18 | all-reduce | flops 257 | bytes 2056 | tf_op jit(solution)/shard_map/psum | solution.py:16
  (137 shorter events, 115.9 us)
Async XLA Ops:
  7.2 181.7 %all-gather.3.cloned.1.call-start = ((), (), s32[]{:S(2)}) async-start(), calls=%async_computation.8 | async-start | bytes 14155776 | tf_op jit(solution)/shard_map/all_gather | solution.py:75
  8.3 9.7 %copy-start.13 = (bf16[1,128,3072]{2,1,0:T(8,128)(2,1)S(1)}, bf16[1,128,3072]{2,1,0:T(8,128)(2,1)}, u32[]{:S(2)}) copy-start(bf16[1,128,3072]{2,1,0:T(8,128)(2,1)} %param.13) | copy-start | bytes 2359300
  9.5 35.9 %all-to-all-start = ((bf16[128,8,384]{0,2,1:T(8,128)(2,1)}), bf16[128,8,384]{0,2,1:T(8,128)(2,1)S(1)}, u32[]{:S(2)}, u32[]{:S(2)}) async-start(bf16[128,8,384]{0,2,1:T(8,128)(2,1)} %bitcast.4), calls=%async_computation | async-start | bytes 1572864 | tf_op jit(solution)/shard_map/all_to_all | solution.py:44
  18.0 33.2 %copy-start.14 = (bf16[1,128,3072]{2,1,0:T(8,128)(2,1)S(1)}, bf16[1,128,3072]{2,1,0:T(8,128)(2,1)}, u32[]{:S(2)}) copy-start(bf16[1,128,3072]{2,1,0:T(8,128)(2,1)} %param.14) | copy-start | bytes 2359300
  45.4 42.6 %copy-start.7 = (bf16[128,8,384]{0,2,1:T(8,128)(2,1)}, bf16[128,8,384]{0,2,1:T(8,128)(2,1)S(1)}, u32[]{:S(2)}) copy-start(bf16[128,8,384]{0,2,1:T(8,128)(2,1)S(1)} %all-to-all-done) | copy-start | bytes 2359300
  45.4 37.0 %all-to-all-start.1 = ((bf16[128,8,384]{0,2,1:T(8,128)(2,1)}), bf16[128,8,384]{0,2,1:T(8,128)(2,1)S(1)}, u32[]{:S(2)}, u32[]{:S(2)}) async-start(bf16[128,8,384]{0,2,1:T(8,128)(2,1)} %bitcast.8), calls=%async_computation.1 | async-start | bytes 1572864 | tf_op jit(solution)/shard_map/all_to_all | solution.py:45
  51.2 36.5 %copy-start.18 = (f32[128]{0:T(128)S(1)}, f32[128]{0:T(128)}, u32[]{:S(2)}) copy-start(f32[128]{0:T(128)} %param.18) | copy-start | bytes 1540
  51.2 36.5 %copy-start.19 = (s32[1,4]{1,0:T(1,128)S(1)}, s32[1,4]{1,0:T(1,128)}, u32[]{:S(2)}) copy-start(s32[1,4]{1,0:T(1,128)} %param.16) | copy-start | bytes 52
  82.4 5.6 %copy-start.11 = (bf16[128,8,384]{0,2,1:T(8,128)(2,1)}, bf16[128,8,384]{0,2,1:T(8,128)(2,1)S(1)}, u32[]{:S(2)}) copy-start(bf16[128,8,384]{0,2,1:T(8,128)(2,1)S(1)} %all-to-all-done.1) | copy-start | bytes 2359300
  82.4 36.3 %all-to-all-start.2 = ((bf16[128,8,384]{0,2,1:T(8,128)(2,1)}), bf16[128,8,384]{0,2,1:T(8,128)(2,1)}, u32[]{:S(2)}, u32[]{:S(2)}) async-start(bf16[128,8,384]{0,2,1:T(8,128)(2,1)} %bitcast.10), calls=%async_computation.2 | async-start | bytes 1572864 | tf_op jit(solution)/shard_map/all_to_all | solution.py:46
  87.7 284.4 %reduce-scatter.2.cloned.1.call-start = ((), (), s32[]{:S(2)}) async-start(), calls=%async_computation.7 | async-start | bytes 4866048 | tf_op jit(solution)/shard_map/reduce_scatter | solution.py:120
  125.7 1.9 copy-start.3
  130.5 3.5 copy-start
  134.0 1.9 copy-start.2
  135.9 2.6 copy-start.1
  141.1 3.5 copy-start
  146.5 2.6 copy-start.1
  289.5 28.7 %all-to-all-start.3 = ((bf16[8,128,384]{1,2,0:T(8,128)(2,1)}), bf16[8,128,384]{1,2,0:T(8,128)(2,1)}, u32[]{:S(2)}, u32[]{:S(2)}) async-start(bf16[8,128,384]{1,2,0:T(8,128)(2,1)} %fusion.47), calls=%async_computation.3 | async-start | bytes 1572864 | tf_op jit(solution)/shard_map/all_to_all | solution.py:110
  296.2 2.0 copy-start.8
  318.2 25.2 %all-to-all-start.4 = ((bf16[8,128,384]{2,1,0:T(8,128)(2,1)}), bf16[8,128,384]{2,1,0:T(8,128)(2,1)S(1)}, u32[]{:S(2)}, u32[]{:S(2)}) async-start(bf16[8,128,384]{2,1,0:T(8,128)(2,1)} %copy.163), calls=%async_computation.4 | async-start | bytes 1572864 | tf_op jit(solution)/shard_map/all_to_all | solution.py:113
  323.4 25.6 %copy-start.5 = (f32[8,128,384]{1,0,2:T(8,128)S(1)}, f32[8,128,384]{1,0,2:T(8,128)}, u32[]{:S(2)}) copy-start(f32[8,128,384]{1,0,2:T(8,128)} %copy-done.4) | copy-start | bytes 4718596
  343.4 5.5 %copy-start.9 = (bf16[8,128,384]{2,1,0:T(8,128)(2,1)}, bf16[8,128,384]{2,1,0:T(8,128)(2,1)S(1)}, u32[]{:S(2)}) copy-start(bf16[8,128,384]{2,1,0:T(8,128)(2,1)S(1)} %all-to-all-done.4) | copy-start | bytes 2359300
  343.4 25.9 %all-to-all-start.5 = ((bf16[8,128,384]{2,1,0:T(8,128)(2,1)}), bf16[8,128,384]{2,1,0:T(8,128)(2,1)}, u32[]{:S(2)}, u32[]{:S(2)}) async-start(bf16[8,128,384]{2,1,0:T(8,128)(2,1)} %copy.165), calls=%async_computation.5 | async-start | bytes 1572864 | tf_op jit(solution)/shard_map/all_to_all | solution.py:116
  353.6 2.4 copy-start.10
  (9 other events, 13.0 us)
Sparse Core Ops, SparseCore 0:
  9.8 179.0 all-gather.2
  200.5 91.9 reduce-scatter.1
where the time goes:
time: 432 us; the launch traced here: 430 us
  waiting for transfers between devices  156 us (36%)
  matrix products  86.1 us (20%)
  local copies, waits for them, and re-layouts  60.2 us (14%)
  blocking collectives  43.5 us (10%)
  starting transfers between devices  36.9 us (9%)
  other arithmetic  26.9 us (6%)
  between operations  17.5 us (4%)
    psum x4, blocking collectives, one_axis_at_a_time(): array = lax.psum(array, axis)  43.5 us
    all_gather x1, waiting for transfers between devices, local(): out_full = lax.all_gather(out_grad[0], 'seq', axis=0, tiled=True)  32.1 us
    all_to_all x1, waiting for transfers between devices, local(): lax.all_to_all(key_rows[0], 'seq', split_axis=1, concat_axis=0, tiled=True)  30 us
    all_to_all x1, waiting for transfers between devices, local(): lax.all_to_all(query_rows[0], 'seq', split_axis=1, concat_axis=0, tiled=T...  26.2 us
    dot_general x2, matrix products, backward_block(): jnp.einsum('hqk,qhd->khd', d_scores, query_block, preferred_element_type=...  20.3 us
    all_to_all x1, waiting for transfers between devices, local(): lax.all_to_all(value_rows[0], 'seq', split_axis=1, concat_axis=0, tiled=T...  19.1 us
    dot_general x2, matrix products, backward_block(): jnp.einsum('hqk,khd->qhd', d_scores, k_norm, preferred_element_type=jnp.f...  19 us
    all_to_all x1, waiting for transfers between devices, local(): lax.all_to_all(key_grad.reshape(total, width), 'seq', split_axis=0, conca...  18.6 us
  transfers between devices with their start and end apart: 8, of which 7 were waited for; matrix products, arithmetic and copies ran while one was open for 35% of the time, Pallas kernels for 0%

commit v1 on v0

--- a/solution.py
+++ b/solution.py
@@ -13,7 +13,7 @@
 
 def one_axis_at_a_time(array, axes):
     for axis in axes:
-        array = lax.psum(array, axis)
+        array = jnp.sum(lax.all_gather(array, axis), axis=0)
     return array
 
 

time: 432 us -> 491 us (1.14)
  blocking collectives: 43.5 us -> 104 us
  waiting for transfers between devices: 156 us -> 145 us
  local copies, waits for them, and re-layouts: 60.2 us -> 68.2 us
    all_gather x0 -> x8, blocking collectives: none -> 67.2 us  [one_axis_at_a_time(): array = jnp.sum(lax.all_gather(array, axis), axis=0)]
    psum x4 -> x0, blocking collectives: 43.5 us -> none  [one_axis_at_a_time(): array = lax.psum(array, axis)]
    unnamed x0 -> x4, blocking collectives: none -> 37.2 us
    all_to_all x1, waiting for transfers between devices: 11.9 us -> 0.01 us  [local(): lax.all_to_all(value_grad.reshape(total, width), 'seq', split_axis=0, con...]
    unnamed x41 -> x63, local copies, waits for them, and re-layouts: 14.8 us -> 22.7 us
  transfers between devices with their start and end apart: 8 -> 8, of which waited for: 7 -> 6; matrix products, arithmetic and copies ran while one was open for 35% -> 33% of each run, Pallas kernels for 0% -> 0%
where the time goes in v1:
time: 491 us; the launch traced here: 489 us
  waiting for transfers between devices  145 us (30%)
  blocking collectives  104 us (21%)
  matrix products  86.1 us (18%)
  local copies, waits for them, and re-layouts  68.2 us (14%)
  starting transfers between devices  36.9 us (8%)
  other arithmetic  28.8 us (6%)
  between operations  17.5 us (4%)
    all_gather x8, blocking collectives, one_axis_at_a_time(): array = jnp.sum(lax.all_gather(array, axis), axis=0)  67.2 us
    unnamed x4, blocking collectives  37.2 us
    all_gather x1, waiting for transfers between devices, local(): out_full = lax.all_gather(out_grad[0], 'seq', axis=0, tiled=True)  32.1 us
    all_to_all x1, waiting for transfers between devices, local(): lax.all_to_all(key_rows[0], 'seq', split_axis=1, concat_axis=0, tiled=True)  30 us
    all_to_all x1, waiting for transfers between devices, local(): lax.all_to_all(query_rows[0], 'seq', split_axis=1, concat_axis=0, tiled=T...  26.2 us
    unnamed x63, local copies, waits for them, and re-layouts  22.7 us
    dot_general x2, matrix products, backward_block(): jnp.einsum('hqk,qhd->khd', d_scores, query_block, preferred_element_type=...  20.3 us
    all_to_all x1, waiting for transfers between devices, local(): lax.all_to_all(value_rows[0], 'seq', split_axis=1, concat_axis=0, tiled=T...  19.1 us
  transfers between devices with their start and end apart: 8, of which 6 were waited for; matrix products, arithmetic and copies ran while one was open for 33% of the time, Pallas kernels for 0%

profile of v1, /device:TPU:32, one launch (start us, length us, event | category | flops | bytes accessed | tf_op | source)
XLA Modules:
  0.0 489.1 jit_solution(17965438755989849213)
XLA Ops:
  9.5 8.6 %all-to-all-start = ((bf16[128,8,384]{0,2,1:T(8,128)(2,1)}), bf16[128,8,384]{0,2,1:T(8,128)(2,1)S(1)}, u32[]{:S(2)}, u32[]{:S(2)}) async-start(bf16[128,8,384]{0,2,1:T(8,128)(2,1)} %bitcast.4), calls=%async_computation | async-start | bytes 1572864 | tf_op jit(solution)/shard_map/all_to_all | solution.py:44
  19.2 26.2 %all-to-all-done = bf16[128,8,384]{0,2,1:T(8,128)(2,1)S(1)} async-done(((bf16[128,8,384]{0,2,1:T(8,128)(2,1)}), bf16[128,8,384]{0,2,1:T(8,128)(2,1)S(1)}, u32[]{:S(2)}, u32[]{:S(2)}) %all-to-all-start) | async-done | bytes 786464 | tf_op jit(solution)/shard_map/all_to_all | solution.py:44
  52.3 30.0 %all-to-all-done.1 = bf16[128,8,384]{0,2,1:T(8,128)(2,1)S(1)} async-done(((bf16[128,8,384]{0,2,1:T(8,128)(2,1)}), bf16[128,8,384]{0,2,1:T(8,128)(2,1)S(1)}, u32[]{:S(2)}, u32[]{:S(2)}) %all-to-all-start.1) | async-done | bytes 786464 | tf_op jit(solution)/shard_map/all_to_all | solution.py:45
  99.7 19.1 %all-to-all-done.2 = bf16[128,8,384]{0,2,1:T(8,128)(2,1)} async-done(((bf16[128,8,384]{0,2,1:T(8,128)(2,1)}), bf16[128,8,384]{0,2,1:T(8,128)(2,1)}, u32[]{:S(2)}, u32[]{:S(2)}) %all-to-all-start.2) | async-done | bytes 786464 | tf_op jit(solution)/shard_map/all_to_all | solution.py:46
  128.8 21.1 %while.27 = (s32[]{:T(128)}, bf16[2,3,512,1024]{3,2,1,0:T(8,128)(2,1)}, bf16[2,512,3,128]{3,1,2,0:T(8,128)(2,1)}, s32[2]{0:T(128)S(1)}, s32[1024]{0:T(1024)S(1)}...) while((s32[]{:T(128)}, ...), condition=%wide.region_6.7_spmd, body=%wide.region_4.6_spmd.sunk | while | flops 817035776 | bytes 85746000 | solution.py:73
  156.8 32.1 %all-gather.19.cloned.1.call-done = bf16[1,1024,6144]{2,1,0:T(8,128)(2,1)} async-done(((bf16[1,128,6144]{2,1,0:T(8,128)(2,1)}), bf16[1,1024,6144]{2,1,0:T(8,128)(2,1)}) %all-gather.19.cloned.1.call-update) | async-done | bytes 12582928 | tf_op jit(solution)/shard_map/all_gather | solution.py:75
  188.9 11.4 %fusion.42 = bf16[384,6144]{0,1:T(8,128)(2,1)} fusion(bf16[1024,384]{0,1:T(8,128)(2,1)} %bitcast.177, bf16[1,1024,6144]{2,1,0:T(8,128)(2,1)} %all-gather.19.cloned.1.call-done), kind=kOutput, calls=%fused_computation.45 | convolution fusion | flops 4834197504 | bytes 18087936 | tf_op jit(solution)/shard_map/dot_general | solution.py:76
  200.3 10.4 %fusion.48 = bf16[1024,384]{0,1:T(8,128)(2,1)} fusion(bf16[384,6144]{1,0:T(8,128)(2,1)} %param.17, bf16[1,1024,6144]{2,1,0:T(8,128)(2,1)} %all-gather.19.cloned.1.call-done), kind=kOutput, calls=%fused_computation.62 | convolution fusion | flops 4832231424 | bytes 18087936 | tf_op jit(solution)/shard_map/dot_general | solution.py:77
  210.8 57.7 %while.28 = (s32[]{:T(128)}, f32[1024,3,128]{0,2,1:T(8,128)}, f32[1024,3,128]{0,2,1:T(8,128)S(1)}, f32[2,512,3,128]{3,1,2,0:T(8,128)}, s32[2]{0:T(128)S(1)}, /*i...) while((s32[]{:T(128)}, f32[1024,3,128]{0,2,1:T(8,128)}, ...), condition=%wide.region_9.10_spmd.clone, body=%wide.region_7.9_spmd.clone.sunk | while | flops 1634210816 | bytes 57019604 | solution.py:102
  217.0 10.2 %bitcast_add_fusion.4 = f32[1024,3,128]{0,2,1:T(8,128)} fusion(f32[1024,3,128]{0,2,1:T(8,128)} %get-tuple-element.516, f32[3,512,1024]{2,1,0:T(8,128)} %fusion.83, bf16[2,3,512,1024]{3,2,1,0:T(8,128)(2,1)} %get-tuple-element.535, s32[]{:T(128)} %get-tuple-element.515, pred[]{:T(512)S(6)} %compare.3, bf16[1024,3,128]{0,2,1:T(8,128)(2,1)} %get-tuple-element.534, ...), kind=kOutput, calls=%fused_computation.26.clone.1 | convolution fusion | flops 414452224 | bytes 22414340 | tf_op jit(solution)/shard_map/while/body/eval_jaxpr/hqk,qhd->khd/dot_general | solution.py:95
  227.2 9.7 %fusion.84 = f32[2,512,3,128]{3,1,2,0:T(8,128)} fusion(f32[2,512,3,128]{3,1,2,0:T(8,128)} %get-tuple-element.518, s32[]{:T(128)} %get-tuple-element.515, bf16[1024,3,128]{2,0,1:T(8,128)(2,1)} %get-tuple-element.538, f32[3,512,1024]{2,1,0:T(8,128)} %fusion.83, bf16[2,3,512,1024]{3,2,1,0:T(8,128)(2,1)} %get-tuple-element.535), kind=kOutput, calls=%fused_computation.28.clone.1 | convolution fusion | flops 413665792 | bytes 20448768 | tf_op jit(solution)/shard_map/while/body/eval_jaxpr/hqk,khd->qhd/dot_general | solution.py:98
  246.1 10.1 %bitcast_add_fusion.4 = f32[1024,3,128]{0,2,1:T(8,128)} fusion(f32[1024,3,128]{0,2,1:T(8,128)} %get-tuple-element.516, f32[3,512,1024]{2,1,0:T(8,128)} %fusion.83, bf16[2,3,512,1024]{3,2,1,0:T(8,128)(2,1)} %get-tuple-element.535, s32[]{:T(128)} %get-tuple-element.515, pred[]{:T(512)S(6)} %compare.3, bf16[1024,3,128]{0,2,1:T(8,128)(2,1)} %get-tuple-element.534, ...), kind=kOutput, calls=%fused_computation.26.clone.1 | convolution fusion | flops 414452224 | bytes 22414340 | tf_op jit(solution)/shard_map/while/body/eval_jaxpr/hqk,qhd->khd/dot_general | solution.py:95
  256.2 9.3 %fusion.84 = f32[2,512,3,128]{3,1,2,0:T(8,128)} fusion(f32[2,512,3,128]{3,1,2,0:T(8,128)} %get-tuple-element.518, s32[]{:T(128)} %get-tuple-element.515, bf16[1024,3,128]{2,0,1:T(8,128)(2,1)} %get-tuple-element.538, f32[3,512,1024]{2,1,0:T(8,128)} %fusion.83, bf16[2,3,512,1024]{3,2,1,0:T(8,128)(2,1)} %get-tuple-element.535), kind=kOutput, calls=%fused_computation.28.clone.1 | convolution fusion | flops 413665792 | bytes 20448768 | tf_op jit(solution)/shard_map/while/body/eval_jaxpr/hqk,khd->qhd/dot_general | solution.py:98
  300.3 17.9 %all-to-all-done.3 = bf16[8,128,384]{1,2,0:T(8,128)(2,1)} async-done(((bf16[8,128,384]{1,2,0:T(8,128)(2,1)}), bf16[8,128,384]{1,2,0:T(8,128)(2,1)}, u32[]{:S(2)}, u32[]{:S(2)}) %all-to-all-start.3) | async-done | bytes 786464 | tf_op jit(solution)/shard_map/all_to_all | solution.py:110
  324.8 18.6 %all-to-all-done.4 = bf16[8,128,384]{2,1,0:T(8,128)(2,1)S(1)} async-done(((bf16[8,128,384]{2,1,0:T(8,128)(2,1)}), bf16[8,128,384]{2,1,0:T(8,128)(2,1)S(1)}, u32[]{:S(2)}, u32[]{:S(2)}) %all-to-all-start.4) | async-done | bytes 786464 | tf_op jit(solution)/shard_map/all_to_all | solution.py:113
  356.0 10.1 %all-gather.9 = f32[4,1,128]{2,1,0:T(1,128)S(1)} all-gather(f32[1,1,128]{2,1,0:T(1,128)S(1)} %bitcast.183), channel_id=3, replica_groups=mesh['dp_0'=4,'dp_1'=4,'dp_2'=2,'seq'=8] {'dp_0'}, dimensions={0}, use_global_device_ids=true | all-gather | bytes 2560 | tf_op jit(solution)/shard_map/all_gather | solution.py:16
  366.1 9.7 %all-gather.10 = f32[4,1,128]{2,1,0:T(1,128)S(1)} all-gather(f32[1,1,128]{2,1,0:T(1,128)S(1)} %bitcast.179), channel_id=4, replica_groups=mesh['dp_0'=4,'dp_1'=4,'dp_2'=2,'seq'=8] {'dp_1'}, dimensions={0}, use_global_device_ids=true | all-gather | bytes 2560 | tf_op jit(solution)/shard_map/all_gather | solution.py:16
  377.6 14.8 %all-gather.12 = f32[8,1,128]{2,1,0:T(1,128)S(1)} all-gather(f32[1,1,128]{2,1,0:T(1,128)S(1)} %bitcast.180), channel_id=6, replica_groups=mesh['dp_0'=4,'dp_1'=4,'dp_2'=2,'seq'=8] {'seq'}, dimensions={0}, use_global_device_ids=true | all-gather | bytes 4608 | tf_op jit(solution)/shard_map/all_gather | solution.py:16
  392.4 7.0 %all-gather.13 = f32[4,1,128]{2,1,0:T(1,128)S(1)} all-gather(f32[1,1,128]{2,1,0:T(1,128)S(1)} %bitcast.178), channel_id=7, replica_groups=mesh['dp_0'=4,'dp_1'=4,'dp_2'=2,'seq'=8] {'dp_0'}, dimensions={0}, use_global_device_ids=true | all-gather | bytes 2560 | tf_op jit(solution)/shard_map/all_gather | solution.py:16
  399.4 7.0 %all-gather.14 = f32[4,1,128]{2,1,0:T(1,128)S(1)} all-gather(f32[1,1,128]{2,1,0:T(1,128)S(1)} %bitcast.181), channel_id=8, replica_groups=mesh['dp_0'=4,'dp_1'=4,'dp_2'=2,'seq'=8] {'dp_1'}, dimensions={0}, use_global_device_ids=true | all-gather | bytes 2560 | tf_op jit(solution)/shard_map/all_gather | solution.py:16
  408.2 15.1 %all-gather.16 = f32[8,1,128]{2,1,0:T(1,128)S(1)} all-gather(f32[1,1,128]{2,1,0:T(1,128)S(1)} %bitcast.182), channel_id=10, replica_groups=mesh['dp_0'=4,'dp_1'=4,'dp_2'=2,'seq'=8] {'seq'}, dimensions={0}, use_global_device_ids=true | all-gather | bytes 4608 | tf_op jit(solution)/shard_map/all_gather | solution.py:16
  430.3 9.8 %all-reduce = f32[4]{0:T(128)S(1)} all-reduce(f32[4]{0:T(128)S(1)} %dynamic-update-slice), channel_id=1, replica_groups=mesh['dp_0'=4,'dp_1'=4,'dp_2'=2,'seq'=8] {'dp_0'}, use_global_device_ids=true, to_apply=%add | all-reduce | flops 4 | bytes 32
  443.2 9.7 %all-reduce.1 = f32[4]{0:T(128)S(1)} all-reduce(f32[4]{0:T(128)S(1)} %dynamic-update-slice.1), channel_id=1, replica_groups=mesh['dp_0'=4,'dp_1'=4,'dp_2'=2,'seq'=8] {'dp_1'}, use_global_device_ids=true, to_apply=%add.1 | all-reduce | flops 4 | bytes 32
  462.1 15.3 %all-reduce.3 = f32[8]{0:T(128)S(1)} all-reduce(f32[8]{0:T(128)S(1)} %dynamic-update-slice.3), channel_id=1, replica_groups=mesh['dp_0'=4,'dp_1'=4,'dp_2'=2,'seq'=8] {'seq'}, use_global_device_ids=true, to_apply=%add.3 | all-reduce | flops 8 | bytes 64
  (179 shorter events, 156.9 us)
Async XLA Ops:
  7.2 181.7 %all-gather.19.cloned.1.call-start = ((), (), s32[]{:S(2)}) async-start(), calls=%async_computation.8 | async-start | bytes 14155776 | tf_op jit(solution)/shard_map/all_gather | solution.py:75
  8.3 9.7 %copy-start.13 = (bf16[1,128,3072]{2,1,0:T(8,128)(2,1)S(1)}, bf16[1,128,3072]{2,1,0:T(8,128)(2,1)}, u32[]{:S(2)}) copy-start(bf16[1,128,3072]{2,1,0:T(8,128)(2,1)} %param.13) | copy-start | bytes 2359300
  9.5 35.9 %all-to-all-start = ((bf16[128,8,384]{0,2,1:T(8,128)(2,1)}), bf16[128,8,384]{0,2,1:T(8,128)(2,1)S(1)}, u32[]{:S(2)}, u32[]{:S(2)}) async-start(bf16[128,8,384]{0,2,1:T(8,128)(2,1)} %bitcast.4), calls=%async_computation | async-start | bytes 1572864 | tf_op jit(solution)/shard_map/all_to_all | solution.py:44
  18.0 33.2 %copy-start.14 = (bf16[1,128,3072]{2,1,0:T(8,128)(2,1)S(1)}, bf16[1,128,3072]{2,1,0:T(8,128)(2,1)}, u32[]{:S(2)}) copy-start(bf16[1,128,3072]{2,1,0:T(8,128)(2,1)} %param.14) | copy-start | bytes 2359300
  45.4 42.7 %copy-start.7 = (bf16[128,8,384]{0,2,1:T(8,128)(2,1)}, bf16[128,8,384]{0,2,1:T(8,128)(2,1)S(1)}, u32[]{:S(2)}) copy-start(bf16[128,8,384]{0,2,1:T(8,128)(2,1)S(1)} %all-to-all-done) | copy-start | bytes 2359300
  45.4 37.0 %all-to-all-start.1 = ((bf16[128,8,384]{0,2,1:T(8,128)(2,1)}), bf16[128,8,384]{0,2,1:T(8,128)(2,1)S(1)}, u32[]{:S(2)}, u32[]{:S(2)}) async-start(bf16[128,8,384]{0,2,1:T(8,128)(2,1)} %bitcast.8), calls=%async_computation.1 | async-start | bytes 1572864 | tf_op jit(solution)/shard_map/all_to_all | solution.py:45
  51.2 36.5 %copy-start.19 = (f32[128]{0:T(128)S(1)}, f32[128]{0:T(128)}, u32[]{:S(2)}) copy-start(f32[128]{0:T(128)} %param.18) | copy-start | bytes 1540
  51.2 36.5 %copy-start.20 = (s32[1,4]{1,0:T(1,128)S(1)}, s32[1,4]{1,0:T(1,128)}, u32[]{:S(2)}) copy-start(s32[1,4]{1,0:T(1,128)} %param.16) | copy-start | bytes 52
  82.4 5.3 %copy-start.11 = (bf16[128,8,384]{0,2,1:T(8,128)(2,1)}, bf16[128,8,384]{0,2,1:T(8,128)(2,1)S(1)}, u32[]{:S(2)}) copy-start(bf16[128,8,384]{0,2,1:T(8,128)(2,1)S(1)} %all-to-all-done.1) | copy-start | bytes 2359300
  82.4 36.3 %all-to-all-start.2 = ((bf16[128,8,384]{0,2,1:T(8,128)(2,1)}), bf16[128,8,384]{0,2,1:T(8,128)(2,1)}, u32[]{:S(2)}, u32[]{:S(2)}) async-start(bf16[128,8,384]{0,2,1:T(8,128)(2,1)} %bitcast.10), calls=%async_computation.2 | async-start | bytes 1572864 | tf_op jit(solution)/shard_map/all_to_all | solution.py:46
  87.7 339.2 %reduce-scatter.2.cloned.1.call-start = ((), (), s32[]{:S(2)}) async-start(), calls=%async_computation.7 | async-start | bytes 4866048 | tf_op jit(solution)/shard_map/reduce_scatter | solution.py:120
  130.5 3.5 copy-start
  141.1 3.5 copy-start
  289.5 28.7 %all-to-all-start.3 = ((bf16[8,128,384]{1,2,0:T(8,128)(2,1)}), bf16[8,128,384]{1,2,0:T(8,128)(2,1)}, u32[]{:S(2)}, u32[]{:S(2)}) async-start(bf16[8,128,384]{1,2,0:T(8,128)(2,1)} %fusion.47), calls=%async_computation.3 | async-start | bytes 1572864 | tf_op jit(solution)/shard_map/all_to_all | solution.py:110
  318.2 25.2 %all-to-all-start.4 = ((bf16[8,128,384]{2,1,0:T(8,128)(2,1)}), bf16[8,128,384]{2,1,0:T(8,128)(2,1)S(1)}, u32[]{:S(2)}, u32[]{:S(2)}) async-start(bf16[8,128,384]{2,1,0:T(8,128)(2,1)} %copy.163), calls=%async_computation.4 | async-start | bytes 1572864 | tf_op jit(solution)/shard_map/all_to_all | solution.py:113
  323.4 25.6 %copy-start.24 = (u32[256]{0:T(256)S(1)}, u32[256]{0:T(256)}, u32[]{:S(2)}) copy-start(u32[256]{0:T(256)} %constant.70) | copy-start | bytes 3076
  323.4 26.1 %copy-start.23 = (u32[256]{0:T(256)S(1)}, u32[256]{0:T(256)}, u32[]{:S(2)}) copy-start(u32[256]{0:T(256)} %constant.75) | copy-start | bytes 3076
  323.4 26.7 %copy-start.22 = (u32[256]{0:T(256)S(1)}, u32[256]{0:T(256)}, u32[]{:S(2)}) copy-start(u32[256]{0:T(256)} %constant.80) | copy-start | bytes 3076
  323.5 27.3 %copy-start.21 = (u32[256]{0:T(256)S(1)}, u32[256]{0:T(256)}, u32[]{:S(2)}) copy-start(u32[256]{0:T(256)} %constant.85) | copy-start | bytes 3076
  323.5 27.9 %copy-start.5 = (f32[8,128,384]{1,0,2:T(8,128)S(1)}, f32[8,128,384]{1,0,2:T(8,128)}, u32[]{:S(2)}) copy-start(f32[8,128,384]{1,0,2:T(8,128)} %copy-done.4) | copy-start | bytes 4718596
  343.4 7.9 %copy-start.9 = (bf16[8,128,384]{2,1,0:T(8,128)(2,1)}, bf16[8,128,384]{2,1,0:T(8,128)(2,1)S(1)}, u32[]{:S(2)}) copy-start(bf16[8,128,384]{2,1,0:T(8,128)(2,1)S(1)} %all-to-all-done.4) | copy-start | bytes 2359300
  343.4 111.5 %all-to-all-start.5 = ((bf16[8,128,384]{2,1,0:T(8,128)(2,1)}), bf16[8,128,384]{2,1,0:T(8,128)(2,1)}, u32[]{:S(2)}, u32[]{:S(2)}) async-start(bf16[8,128,384]{2,1,0:T(8,128)(2,1)} %copy.165), calls=%async_computation.5 | async-start | bytes 1572864 | tf_op jit(solution)/shard_map/all_to_all | solution.py:116
  356.0 73.9 %copy-start.10 = (bf16[8,128,384]{2,1,0:T(8,128)(2,1)S(1)}, bf16[8,128,384]{2,1,0:T(8,128)(2,1)}, u32[]{:S(2)}) copy-start(bf16[8,128,384]{2,1,0:T(8,128)(2,1)} %copy-done.9) | copy-start | bytes 2359300
  454.9 25.5 %copy-start.17 = (bf16[384,192]{0,1:T(8,128)(2,1)S(1)}, bf16[384,192]{0,1:T(8,128)(2,1)}, u32[]{:S(2)}) copy-start(bf16[384,192]{0,1:T(8,128)(2,1)} %reduce-scatter.2.cloned.1.call-done) | copy-start | bytes 442372
  (14 other events, 24.1 us)
Sparse Core Ops, SparseCore 0:
  9.8 179.0 all-gather.18
  200.5 91.9 reduce-scatter.1
